TPU v7x, 256 devices: a whole 4x4x8 slice. The times are simulated.
256 devices in a mesh: layer: 8 (over y, z_lo), lat: 4 (over x), tok: 8 (over z_hi, core).
Axes of the slice: x: 4, y: 4, z: 8 (z_hi: 4, z_lo: 2; z = z_hi * 2 + z_lo), core: 2. Of those that a mesh axis runs over, the one named last changes fastest.
Arguments:
- mlp_inputs: bfloat16 [8, 768, 4096], P('layer', ('lat', 'tok')), may hold values from -6 to 6
- mlp_outputs: bfloat16 [8, 768, 4096], P('layer', ('lat', 'tok')), may hold values from -6 to 6
- encoder: bfloat16 [8, 4096, 16384], P('layer', None, ('lat', 'tok')), may hold values from -0.09375 to 0.09375
- encoder_bias: float32 [8, 16384], P('layer', ('lat', 'tok')), may hold values from -3 to 3
- active_words: int32 [8, 768, 1024], P('layer', None, ('lat', 'tok')), may hold values from 0 to 65535
- decoder: bfloat16 [8, 16384, 4096], P('layer', ('lat', 'tok')), may hold values from -0.0234375 to 0.0234375
Outputs:
- reconstruction_error: bfloat16 [8, 768, 4096], P('layer', ('lat', 'tok'))
- decoder_grad: bfloat16 [8, 16384, 4096], P('layer', ('lat', 'tok'))
Inputs may be any that keep to these rules, and one draw needn't show every extreme that they name: `active_words`: each word holds 16 independent gate decisions of one token in its low 16 bits.
All inputs are finite; a program needn't handle non-finite values.
Results may differ from a plain program's by a relative error of at most 0.0037.
Values may be sent and summed in bfloat16 or wider, within the bound.
No kernel may reach another device: no remote copies, remote signals or barrier semaphores. Data moves between devices by JAX's collectives and lax.ppermute only.
A program may use at most 128 MiB of HBM per device.

v0:
```python
import jax
import jax.numpy as jnp
from jax import lax
from jax.sharding import Mesh
from jax.sharding import PartitionSpec as P

LAYER = ("layer_0", "layer_1")


def whole_of(x, axes, dim):
    if not axes:
        return x
    nearer = lax.all_gather(x, axes[-1], axis=dim, tiled=True)
    return whole_of(nearer, axes[:-1], dim)


def unpack_words(words):
    shifts = jnp.arange(16, dtype=jnp.int32)
    bits = jnp.right_shift(words[..., None], shifts) & 1
    return bits.reshape(words.shape[:-1] + (words.shape[-1] * 16,)).astype(jnp.float32)


def local(mlp_inputs, mlp_outputs, encoder, encoder_bias, active_words, decoder):
    weights_in = encoder[0]
    bias_row = encoder_bias[0]
    words = active_words[0]
    weights_out = decoder[0]
    before_gate = (
        jnp.dot(
            lax.all_gather(mlp_inputs[0], ("lat", "tok"), axis=0, tiled=True),
            weights_in,
            preferred_element_type=jnp.float32,
        )
        + bias_row[None, :]
    )
    latent = (unpack_words(words) * before_gate).astype(jnp.bfloat16)
    write = lax.psum_scatter(
        jnp.dot(latent, weights_out, preferred_element_type=jnp.float32),
        ("lat", "tok"),
        scatter_dimension=0,
        tiled=True,
    )
    target = mlp_outputs[0].astype(jnp.float32)
    layer_index = lax.axis_index(LAYER)
    piece = whole_of(write[None], LAYER, 0)
    levels = jnp.arange(piece.shape[0], dtype=jnp.int32)
    keep = (levels <= layer_index).astype(jnp.float32)
    recon = jnp.sum(piece * keep[:, None, None], axis=0)
    difference = recon - target
    piece = lax.all_gather(difference[None], LAYER, axis=0, tiled=True)
    levels = jnp.arange(piece.shape[0], dtype=jnp.int32)
    keep = (levels >= layer_index).astype(jnp.float32)
    later = jnp.sum(piece * keep[:, None, None], axis=0)
    signal = later.astype(jnp.bfloat16)
    tokens_all = latent.shape[0]
    gathered = lax.all_gather(signal, ("lat", "tok"), axis=0, tiled=True)
    total = lax.dot_general(
        latent, gathered, (((0,), (0,)), ((), ())), preferred_element_type=jnp.float32
    )
    grad_block = (total / tokens_all).astype(jnp.bfloat16)
    return (difference.astype(jnp.bfloat16)[None], grad_block[None])


def solution(mesh):
    split = Mesh(
        mesh.devices.reshape(4, 2, mesh.shape["lat"], mesh.shape["tok"]),
        ("layer_0", "layer_1", "lat", "tok"),
    )
    placed = (
        P(LAYER, ("lat", "tok"), None),
        P(LAYER, ("lat", "tok"), None),
        P(LAYER, None, ("lat", "tok")),
        P(LAYER, ("lat", "tok")),
        P(LAYER, None, ("lat", "tok")),
        P(LAYER, ("lat", "tok"), None),
    )
    return jax.shard_map(
        local,
        mesh=split,
        in_specs=placed,
        out_specs=(P(LAYER, ("lat", "tok"), None), P(LAYER, ("lat", "tok"), None)),
        check_vma=False,
    )
```

profile of v0, /device:TPU:1, one launch (start us, length us, event | category | flops | bytes accessed | tf_op | source)
XLA Modules:
  0.0 454.7 jit_solution(15112110966650471053)
XLA Ops:
  7.2 0.0 copy-start.2
  7.2 0.0 all-gather.13.cloned.1.call-start
  7.2 0.7 all-gather.13.cloned.1.call-update
  7.9 0.0 reduce-scatter.2.cloned.1.call-start
  8.0 1.0 shift_right_arithmetic.23
  9.0 0.5 copy.10
  9.5 0.1 shift_right_arithmetic.26
  9.5 74.2 %all-gather.13.cloned.1.call-done = bf16[1,768,4096]{2,1,0:T(8,128)(2,1)} async-done(((bf16[1,24,4096]{2,1,0:T(8,128)(2,1)}), bf16[1,768,4096]{2,1,0:T(8,128)(2,1)}) %all-gather.13.cloned.1.call-update) | async-done | bytes 6291472 | tf_op jit(solution)/shard_map/all_gather | solution.py:30
  83.7 0.0 copy-done.2
  83.7 0.0 copy-start.1
  83.7 7.6 %multiply_convert_fusion.1 = bf16[768,512]{1,0:T(8,128)(2,1)S(1)} fusion(s32[768,512]{1,0:T(8,128)S(1)} %copy.10, bf16[1,4096,512]{2,1,0:T(8,128)(2,1)} %param.8, bf16[1,768,4096]{2,1,0:T(8,128)(2,1)} %all-gather.13.cloned.1.call-done, f32[512]{0:T(512)S(1)} %bitcast.28, s32[512]{0:T(512)S(1)} %shift_right_arithmetic.26), kind=kOutput, calls=%fused_computation.9 | convolution fusion | flops 3223584768 | bytes 12849152 | tf_op jit(solution)/shard_map/dot_general | solution.py:29
  91.3 0.0 copy-done.1
  91.3 6.4 %fusion.3 = f32[768,4096]{1,0:T(8,128)} fusion(bf16[768,512]{1,0:T(8,128)(2,1)S(1)} %multiply_convert_fusion.1, bf16[1,512,4096]{2,1,0:T(8,128)(2,1)S(1)} %copy-done.1), kind=kOutput, calls=%fused_computation.4 | convolution fusion | flops 3221225472 | bytes 17563648 | tf_op jit(solution)/shard_map/dot_general | solution.py:38
  97.8 0.0 reduce-scatter.2.cloned.1.call-update
  97.8 0.0 copy-start
  97.8 0.0 all-gather.7.cloned.1.call-start
  97.9 139.6 %reduce-scatter.2.cloned.1.call-done = f32[24,4096]{1,0:T(8,128)} async-done(((f32[768,4096]{1,0:T(8,128)}), f32[24,4096]{1,0:T(8,128)}) %reduce-scatter.2.cloned.1.call-update) | async-done | bytes 393232 | tf_op jit(solution)/shard_map/reduce_scatter | solution.py:37
  237.5 10.7 %all-gather.1 = f32[48,4096]{1,0:T(8,128)} all-gather(f32[24,4096]{1,0:T(8,128)} %reduce-scatter.2.cloned.1.call-done), channel_id=3, replica_groups=mesh['layer_0'=4,'layer_1'=2,'lat'=4,'tok'=8] {'layer_1'}, dimensions={0}, use_global_device_ids=true | all-gather | bytes 1179648 | tf_op jit(solution)/shard_map/all_gather | solution.py:13
  248.2 0.0 all-gather.7.cloned.1.call-update
  248.3 0.0 all-gather.9.cloned.1.call-start
  248.3 42.3 %all-gather.7.cloned.1.call-done = f32[8,24,4096]{2,1,0:T(8,128)} async-done(((f32[2,24,4096]{2,1,0:T(8,128)}), f32[8,24,4096]{2,1,0:T(8,128)}) %all-gather.7.cloned.1.call-update) | async-done | bytes 3145744 | tf_op jit(solution)/shard_map/all_gather | solution.py:13
  290.6 2.3 multiply_reduce_fusion.1
  292.9 0.0 copy-done
  292.9 0.9 fusion.10
  293.7 0.0 all-gather.9.cloned.1.call-update
  293.8 0.0 all-gather.11.cloned.1.call-start
  293.8 74.1 %all-gather.9.cloned.1.call-done = f32[8,24,4096]{2,1,0:T(8,128)} async-done(((f32[1,24,4096]{2,1,0:T(8,128)}), f32[8,24,4096]{2,1,0:T(8,128)}) %all-gather.9.cloned.1.call-update) | async-done | bytes 3145744 | tf_op jit(solution)/shard_map/all_gather | solution.py:50
  367.9 2.9 multiply_reduce_fusion
  370.8 0.0 all-gather.11.cloned.1.call-update
  370.9 69.5 %all-gather.11.cloned.1.call-done = bf16[768,4096]{1,0:T(8,128)(2,1)} async-done(((bf16[24,4096]{1,0:T(8,128)(2,1)}), bf16[768,4096]{1,0:T(8,128)(2,1)}) %all-gather.11.cloned.1.call-update) | async-done | bytes 6291472 | tf_op jit(solution)/shard_map/all_gather | solution.py:56
  440.3 7.9 %fusion.2 = bf16[1,512,4096]{2,1,0:T(8,128)(2,1)} fusion(bf16[768,512]{1,0:T(8,128)(2,1)S(1)} %multiply_convert_fusion.1, bf16[768,4096]{1,0:T(8,128)(2,1)} %all-gather.11.cloned.1.call-done), kind=kOutput, calls=%fused_computation.3 | convolution fusion | flops 3225419776 | bytes 11272192 | tf_op jit(solution)/shard_map/dot_general | solution.py:57
  (3 shorter events, 0.0 us)
Async XLA Ops:
  7.2 76.6 %copy-start.2 = (f32[1,512]{1,0:T(1,128)S(1)}, f32[1,512]{1,0:T(1,128)}, u32[]{:S(2)}) copy-start(f32[1,512]{1,0:T(1,128)} %param.9) | copy-start | bytes 6148
  7.2 76.6 %all-gather.13.cloned.1.call-start = ((), (), s32[]{:S(2)}) async-start(), calls=%async_computation.5 | async-start | bytes 6488064 | tf_op jit(solution)/shard_map/all_gather | solution.py:30
  7.9 229.6 %reduce-scatter.2.cloned.1.call-start = ((), (), s32[]{:S(2)}) async-start(), calls=%async_computation.1 | async-start | bytes 12976128 | tf_op jit(solution)/shard_map/reduce_scatter | solution.py:37
  83.7 7.6 %copy-start.1 = (bf16[1,512,4096]{2,1,0:T(8,128)(2,1)S(1)}, bf16[1,512,4096]{2,1,0:T(8,128)(2,1)}, u32[]{:S(2)}) copy-start(bf16[1,512,4096]{2,1,0:T(8,128)(2,1)} %param.11) | copy-start | bytes 12582916
  97.8 195.1 %copy-start = (bf16[1,24,4096]{2,1,0:T(8,128)(2,1)S(1)}, bf16[1,24,4096]{2,1,0:T(8,128)(2,1)}, u32[]{:S(2)}) copy-start(bf16[1,24,4096]{2,1,0:T(8,128)(2,1)} %param.7) | copy-start | bytes 589828
  97.8 192.8 %all-gather.7.cloned.1.call-start = ((), (), s32[]{:S(2)}) async-start(), calls=%async_computation.2 | async-start | bytes 3932160 | tf_op jit(solution)/shard_map/all_gather | solution.py:13
  248.3 119.6 %all-gather.9.cloned.1.call-start = ((), (), s32[]{:S(2)}) async-start(), calls=%async_computation.3 | async-start | bytes 3538944 | tf_op jit(solution)/shard_map/all_gather | solution.py:50
  293.8 146.5 %all-gather.11.cloned.1.call-start = ((), (), s32[]{:S(2)}) async-start(), calls=%async_computation.4 | async-start | bytes 6488064 | tf_op jit(solution)/shard_map/all_gather | solution.py:56
Sparse Core Ops, SparseCore 0:
  10.5 73.1 all-gather.12
  97.9 139.5 reduce-scatter.1
  248.4 42.2 all-gather.6
  293.9 73.9 all-gather.8
  371.0 69.2 all-gather.10
where the time goes:
time: 455 us
  waiting for transfers between devices  400 us (88%)
  matrix products  21.9 us (5%)
  between operations  13.9 us (3%)
  blocking collectives  10.7 us (2%)
  other arithmetic  6.06 us (1%)
    reduce_scatter x1, waiting for transfers between devices, local(): lax.psum_scatter(jnp.dot(latent, weights_out, preferred_element_type=jnp....  140 us
    all_gather x1, waiting for transfers between devices, local(): lax.all_gather(mlp_inputs[0], ('lat', 'tok'), axis=0, tiled=True)  74.2 us
    all_gather x1, waiting for transfers between devices, local(): piece = lax.all_gather(difference[None], LAYER, axis=0, tiled=True)  74.1 us
    all_gather x1, waiting for transfers between devices, local(): gathered = lax.all_gather(signal, ('lat', 'tok'), axis=0, tiled=True)  69.5 us
    all_gather x1, waiting for transfers between devices, whole_of(): nearer = lax.all_gather(x, axes[-1], axis=dim, tiled=True)  42.3 us
    all_gather x1, blocking collectives, whole_of(): nearer = lax.all_gather(x, axes[-1], axis=dim, tiled=True)  10.7 us
  transfers between devices with their start and end apart: 5, of which 5 were waited for; matrix products, arithmetic and copies ran while one was open for 0% of the time, Pallas kernels for 0%

commit v1 on v0

--- a/solution.py
+++ b/solution.py
@@ -5,6 +5,11 @@
 from jax.sharding import PartitionSpec as P
 
 LAYER = ("layer_0", "layer_1")
+
+
+def all_by_exchange(array, name, dim):
+    sent = jnp.stack([array] * lax.axis_size(name))
+    return jnp.concatenate(lax.all_to_all(sent, name, 0, 0), axis=dim)
 
 
 def whole_of(x, axes, dim):
@@ -47,7 +52,7 @@
     keep = (levels <= layer_index).astype(jnp.float32)
     recon = jnp.sum(piece * keep[:, None, None], axis=0)
     difference = recon - target
-    piece = lax.all_gather(difference[None], LAYER, axis=0, tiled=True)
+    piece = all_by_exchange(difference[None], LAYER, 0)
     levels = jnp.arange(piece.shape[0], dtype=jnp.int32)
     keep = (levels >= layer_index).astype(jnp.float32)
     later = jnp.sum(piece * keep[:, None, None], axis=0)

time: 455 us -> 423 us (0.930)
  waiting for transfers between devices: 400 us -> 364 us
    all_gather x1 -> x0, waiting for transfers between devices: 74.1 us -> none  [local(): piece = lax.all_gather(difference[None], LAYER, axis=0, tiled=True)]
    all_to_all x0 -> x1, waiting for transfers between devices: none -> 37.1 us  [all_by_exchange(): return jnp.concatenate(lax.all_to_all(sent, name, 0, 0), axis=dim)]
where the time goes in v1:
time: 423 us
  waiting for transfers between devices  364 us (86%)
  matrix products  22.6 us (5%)
  between operations  13.9 us (3%)
  blocking collectives  10.6 us (3%)
    reduce_scatter x1, waiting for transfers between devices, local(): lax.psum_scatter(jnp.dot(latent, weights_out, preferred_element_type=jnp....  140 us
    all_gather x1, waiting for transfers between devices, local(): lax.all_gather(mlp_inputs[0], ('lat', 'tok'), axis=0, tiled=True)  74.2 us
    all_gather x1, waiting for transfers between devices, local(): gathered = lax.all_gather(signal, ('lat', 'tok'), axis=0, tiled=True)  70.3 us
    all_gather x1, waiting for transfers between devices, whole_of(): nearer = lax.all_gather(x, axes[-1], axis=dim, tiled=True)  42.2 us
    all_to_all x1, waiting for transfers between devices, all_by_exchange(): return jnp.concatenate(lax.all_to_all(sent, name, 0, 0), axis=dim)  37.1 us
    all_gather x1, blocking collectives, whole_of(): nearer = lax.all_gather(x, axes[-1], axis=dim, tiled=True)  10.6 us
    dot_general x1, matrix products, local(): lax.dot_general(latent, gathered, (((0,), (0,)), ((), ())), preferred_ele...  8.56 us
  transfers between devices with their start and end apart: 5, of which 5 were waited for; matrix products, arithmetic and copies ran while one was open for 0% of the time, Pallas kernels for 0%

profile of v1, /device:TPU:1, one launch (start us, length us, event | category | flops | bytes accessed | tf_op | source)
XLA Modules:
  0.0 423.1 jit_solution(4065091434473498682)
XLA Ops:
  7.2 0.0 copy-start.2
  7.2 0.0 all-gather.10.cloned.1.call-start
  7.2 0.7 all-gather.10.cloned.1.call-update
  7.9 0.0 reduce-scatter.2.cloned.1.call-start
  8.0 1.0 shift_right_arithmetic.23
  9.0 0.5 copy.12
  9.5 0.1 shift_right_arithmetic.26
  9.5 74.2 %all-gather.10.cloned.1.call-done = bf16[1,768,4096]{2,1,0:T(8,128)(2,1)} async-done(((bf16[1,24,4096]{2,1,0:T(8,128)(2,1)}), bf16[1,768,4096]{2,1,0:T(8,128)(2,1)}) %all-gather.10.cloned.1.call-update) | async-done | bytes 6291472 | tf_op jit(solution)/shard_map/all_gather | solution.py:35
  83.7 0.0 copy-done.2
  83.7 0.0 copy-start.1
  83.7 7.6 %multiply_convert_fusion.1 = bf16[768,512]{1,0:T(8,128)(2,1)S(1)} fusion(s32[768,512]{1,0:T(8,128)S(1)} %copy.12, bf16[1,4096,512]{2,1,0:T(8,128)(2,1)} %param.8, bf16[1,768,4096]{2,1,0:T(8,128)(2,1)} %all-gather.10.cloned.1.call-done, f32[512]{0:T(512)S(1)} %bitcast.37, s32[512]{0:T(512)S(1)} %shift_right_arithmetic.26), kind=kOutput, calls=%fused_computation.10 | convolution fusion | flops 3223584768 | bytes 12849152 | tf_op jit(solution)/shard_map/dot_general | solution.py:34
  91.3 0.0 copy-done.1
  91.3 0.0 copy-start.3
  91.4 6.4 %fusion.3 = f32[768,4096]{1,0:T(8,128)} fusion(bf16[768,512]{1,0:T(8,128)(2,1)S(1)} %multiply_convert_fusion.1, bf16[1,512,4096]{2,1,0:T(8,128)(2,1)S(1)} %copy-done.1), kind=kOutput, calls=%fused_computation.4 | convolution fusion | flops 3221225472 | bytes 17563648 | tf_op jit(solution)/shard_map/dot_general | solution.py:43
  97.8 0.0 copy-done.3
  97.8 0.0 reduce-scatter.2.cloned.1.call-update
  97.8 0.0 copy-start
  97.8 0.0 all-gather.6.cloned.1.call-start
  97.9 139.9 %reduce-scatter.2.cloned.1.call-done = f32[24,4096]{1,0:T(8,128)} async-done(((f32[768,4096]{1,0:T(8,128)}), f32[24,4096]{1,0:T(8,128)}) %reduce-scatter.2.cloned.1.call-update) | async-done | bytes 393232 | tf_op jit(solution)/shard_map/reduce_scatter | solution.py:42
  237.8 10.6 %all-gather.1 = f32[48,4096]{1,0:T(8,128)} all-gather(f32[24,4096]{1,0:T(8,128)} %reduce-scatter.2.cloned.1.call-done), channel_id=3, replica_groups=mesh['layer_0'=4,'layer_1'=2,'lat'=4,'tok'=8] {'layer_1'}, dimensions={0}, use_global_device_ids=true | all-gather | bytes 1179648 | tf_op jit(solution)/shard_map/all_gather | solution.py:18
  248.4 0.0 all-gather.6.cloned.1.call-update
  248.4 42.2 %all-gather.6.cloned.1.call-done = f32[8,24,4096]{2,1,0:T(8,128)} async-done(((f32[2,24,4096]{2,1,0:T(8,128)}), f32[8,24,4096]{2,1,0:T(8,128)}) %all-gather.6.cloned.1.call-update) | async-done | bytes 3145744 | tf_op jit(solution)/shard_map/all_gather | solution.py:18
  290.7 2.3 multiply_reduce_fusion
  292.9 0.0 copy-done
  292.9 0.7 fusion.11
  293.7 2.0 stack.3
  295.7 3.9 all-to-all-start
  299.6 0.0 all-gather.8.cloned.1.call-start
  299.6 37.1 %all-to-all-done = f32[8,1,24,4096]{3,2,1,0:T(8,128)S(1)} async-done(((f32[8,1,24,4096]{3,2,1,0:T(8,128)}), f32[8,1,24,4096]{3,2,1,0:T(8,128)S(1)}, u32[]{:S(2)}, u32[]{:S(2)}) %all-to-all-start) | async-done | bytes 3145760 | tf_op jit(solution)/shard_map/all_to_all | solution.py:12
  336.8 1.0 fusion.6
  337.7 0.0 all-gather.8.cloned.1.call-update
  337.8 70.3 %all-gather.8.cloned.1.call-done = bf16[768,4096]{1,0:T(8,128)(2,1)} async-done(((bf16[24,4096]{1,0:T(8,128)(2,1)}), bf16[768,4096]{1,0:T(8,128)(2,1)}) %all-gather.8.cloned.1.call-update) | async-done | bytes 6291472 | tf_op jit(solution)/shard_map/all_gather | solution.py:61
  408.0 8.6 %fusion.2 = bf16[1,512,4096]{2,1,0:T(8,128)(2,1)} fusion(bf16[768,512]{1,0:T(8,128)(2,1)} %copy-done.3, bf16[768,4096]{1,0:T(8,128)(2,1)} %all-gather.8.cloned.1.call-done), kind=kOutput, calls=%fused_computation.3 | convolution fusion | flops 3225419776 | bytes 11272192 | tf_op jit(solution)/shard_map/dot_general | solution.py:62
  (3 shorter events, 0.0 us)
Async XLA Ops:
  7.2 76.6 %copy-start.2 = (f32[1,512]{1,0:T(1,128)S(1)}, f32[1,512]{1,0:T(1,128)}, u32[]{:S(2)}) copy-start(f32[1,512]{1,0:T(1,128)} %param.9) | copy-start | bytes 6148
  7.2 76.6 %all-gather.10.cloned.1.call-start = ((), (), s32[]{:S(2)}) async-start(), calls=%async_computation.5 | async-start | bytes 6488064 | tf_op jit(solution)/shard_map/all_gather | solution.py:35
  7.9 229.9 %reduce-scatter.2.cloned.1.call-start = ((), (), s32[]{:S(2)}) async-start(), calls=%async_computation.2 | async-start | bytes 12976128 | tf_op jit(solution)/shard_map/reduce_scatter | solution.py:42
  83.7 7.6 %copy-start.1 = (bf16[1,512,4096]{2,1,0:T(8,128)(2,1)S(1)}, bf16[1,512,4096]{2,1,0:T(8,128)(2,1)}, u32[]{:S(2)}) copy-start(bf16[1,512,4096]{2,1,0:T(8,128)(2,1)} %param.11) | copy-start | bytes 12582916
  91.3 6.4 %copy-start.3 = (bf16[768,512]{1,0:T(8,128)(2,1)}, bf16[768,512]{1,0:T(8,128)(2,1)S(1)}, u32[]{:S(2)}) copy-start(bf16[768,512]{1,0:T(8,128)(2,1)S(1)} %multiply_convert_fusion.1) | copy-start | bytes 2359300
  97.8 195.1 %copy-start = (bf16[1,24,4096]{2,1,0:T(8,128)(2,1)S(1)}, bf16[1,24,4096]{2,1,0:T(8,128)(2,1)}, u32[]{:S(2)}) copy-start(bf16[1,24,4096]{2,1,0:T(8,128)(2,1)} %param.7) | copy-start | bytes 589828
  97.8 192.8 %all-gather.6.cloned.1.call-start = ((), (), s32[]{:S(2)}) async-start(), calls=%async_computation.3 | async-start | bytes 3932160 | tf_op jit(solution)/shard_map/all_gather | solution.py:18
  295.7 41.1 %all-to-all-start = ((f32[8,1,24,4096]{3,2,1,0:T(8,128)}), f32[8,1,24,4096]{3,2,1,0:T(8,128)S(1)}, u32[]{:S(2)}, u32[]{:S(2)}) async-start(f32[8,1,24,4096]{3,2,1,0:T(8,128)} %stack.3), calls=%async_computation.1 | async-start | bytes 6291456 | tf_op jit(solution)/shard_map/all_to_all | solution.py:12
  299.6 108.5 %all-gather.8.cloned.1.call-start = ((), (), s32[]{:S(2)}) async-start(), calls=%async_computation.4 | async-start | bytes 6488064 | tf_op jit(solution)/shard_map/all_gather | solution.py:61
Sparse Core Ops, SparseCore 0:
  10.5 73.1 all-gather.9
  97.9 139.8 reduce-scatter.1
  248.5 42.0 all-gather.5
  337.9 70.1 all-gather.7
